TPU v7x, 256 devices: a whole 4x4x8 slice. The times are simulated.
256 devices in a mesh: tok: 4 (over y), col: 64 (over z, x, core).
Axes of the slice: x: 4, y: 4, z: 8, core: 2. Of those that a mesh axis runs over, the one named last changes fastest.
Arguments:
- row_bank: bfloat16 [16384, 8192], P(None, 'col'), may hold values from -50 to 50
- token_ids: int32 [6144], P('tok'), may hold values from 0 to 16383
- sign_flips: int32 [8192], P('col'), may hold values from -1 to 1, as said below
- damping: float32 [1], replicated, may hold values from 0.1 to 1
Outputs:
- hessian: float32 [8192, 8192], P('tok', 'col')
Inputs may be any that keep to these rules, and one draw needn't show every extreme that they name: `sign_flips`: each entry is -1 or 1.
All inputs are finite; a program needn't handle non-finite values.
Results may differ from a plain program's by a relative error of at most 0.0003.
The roundings to bfloat16 on the way count: a program that leaves them out, or rounds other values in their place, can miss the bound.
Values may be sent and summed in bfloat16 or wider, within the bound.
A program may use at most 128 MiB of HBM per device.

v0:
```python
import math

import jax
import jax.numpy as jnp
from jax import lax
from jax.sharding import Mesh
from jax.sharding import PartitionSpec as P

D = 8192
BLOCK = 32
COL = ("col_0", "col_1", "col_2")
TOK_COL = ("tok", "col_0", "col_1", "col_2")


def grouped_exchange(x, axis, split_dim, concat_dim, work, item_dim, out_dim):
    items = jax.tree.leaves(x)[0].shape[item_dim]
    count = 2 if items % 2 == 0 else 1
    outs = []
    for k in range(count):
        group = jax.tree.map(
            lambda a: lax.slice_in_dim(
                a, k * (items // count), (k + 1) * (items // count), axis=item_dim
            ),
            x,
        )
        outs.append(
            work(
                lax.all_to_all(
                    group, axis, split_axis=split_dim, concat_axis=concat_dim, tiled=True
                )
            )
        )
    return jax.tree.map(lambda *parts: jnp.concatenate(parts, axis=out_dim), *outs)


def by_axis(x, axes):
    for axis in axes:
        x = lax.psum(x, axis)
    return x


def hadamard(order):
    index_range = jnp.arange(order, dtype=jnp.int32)
    anded = jnp.bitwise_and(index_range[:, None], index_range[None, :])
    parity = jnp.zeros((order, order), jnp.int32)
    for bit_place in range(int(order).bit_length()):
        parity = parity + jnp.bitwise_and(jnp.right_shift(anded, bit_place), 1)
    return (1 - 2 * jnp.bitwise_and(parity, 1)).astype(jnp.bfloat16)


def shards(row_bank, token_ids, sign_flips, damping):
    col_width = row_bank.shape[1]
    col_count = lax.axis_size(COL)
    tok_count = lax.axis_size("tok")
    tok_rows = token_ids.shape[0]
    groups = D // BLOCK
    scale = 1.0 / math.sqrt(D)
    inner_table = hadamard(BLOCK)
    outer_table = hadamard(groups)
    col_start = lax.axis_index(COL) * col_width
    picked = jnp.take(row_bank, token_ids, axis=0) * sign_flips.astype(jnp.bfloat16)[None, :]

    def turn_outer(block):
        shaped = block.reshape(block.shape[0], groups, BLOCK)
        turned = (
            jnp.einsum("rab,ac->rcb", shaped, outer_table, preferred_element_type=jnp.float32)
            * scale
        )
        return turned.astype(jnp.bfloat16).reshape(block.shape)

    shaped = picked.reshape(picked.shape[0], -1, BLOCK)
    turned = jnp.einsum("rab,bc->rac", shaped, inner_table, preferred_element_type=jnp.float32)
    half_turned = turned.astype(jnp.bfloat16).reshape(picked.shape)
    grouped = half_turned.reshape(col_count, tok_rows // col_count, col_width)

    def finish(received):
        return turn_outer(received[0])[None]

    finished = grouped_exchange(grouped, COL, 0, 2, finish, 1, 1)
    squares = jnp.sum(jnp.square(finished.astype(jnp.float32)))
    tokens_all = tok_rows * tok_count
    square_sum = by_axis(squares, TOK_COL)
    mean_diag = square_sum / tokens_all / D
    flat = lax.all_gather(finished, COL, axis=1, tiled=True).reshape(-1, D)
    own_cols = lax.dynamic_slice_in_dim(flat, col_start, col_width, 1)
    partial_sum = lax.dot_general(
        flat, own_cols, (((0,), (0,)), ((), ())), preferred_element_type=jnp.float32
    )
    gram_block = lax.psum_scatter(partial_sum, "tok", scatter_dimension=0, tiled=True) / tokens_all
    block_rows = gram_block.shape[0]
    row_index = lax.axis_index("tok") * block_rows + lax.broadcasted_iota(
        jnp.int32, gram_block.shape, 0
    )
    col_index = col_start + lax.broadcasted_iota(jnp.int32, gram_block.shape, 1)
    on_diag = (row_index == col_index).astype(jnp.float32)
    return gram_block + damping[0] * mean_diag * on_diag


def solution(mesh):
    split = Mesh(
        mesh.devices.reshape(mesh.shape["tok"], 8, 4, 2), ("tok", "col_0", "col_1", "col_2")
    )
    in_specs = (P(None, COL), P("tok"), P(COL), P())
    out_specs = P("tok", COL)
    return jax.shard_map(
        shards, mesh=split, in_specs=in_specs, out_specs=out_specs, check_vma=False
    )
```

profile of v0, /device:TPU:1, one launch (start us, length us, event | category | flops | bytes accessed | tf_op | source)
XLA Modules:
  0.0 249.9 jit_solution(16534294959864391081)
XLA Ops:
  6.5 0.7 compare_select_fusion
  7.2 0.7 compare_and_fusion
  7.9 5.4 %gather_fusion = bf16[1536,128]{1,0:T(8,128)(2,1)S(1)} fusion(bf16[16384,128]{1,0:T(8,128)(2,1)} %param.4, s32[2048]{0:T(1024)S(1)} %pad_clamp_fusion), kind=kCustom, calls=%fused_computation | custom fusion | bytes 792576 | tf_op jit(solution)/shard_map/jit(_take)/gather | solution.py:61
  13.3 0.2 copy.6
  13.5 0.7 convert_element_type.39
  14.3 0.3 convolution_convert_fusion
  14.6 1.0 copy.7
  15.6 0.8 reshape_reshape.3
  16.4 0.8 fusion.47
  17.2 25.8 %all_to_all.30 = bf16[64,12,128]{2,1,0:T(8,128)(2,1)S(1)} all-to-all(bf16[64,12,128]{2,1,0:T(8,128)(2,1)S(1)} %get-tuple-element.7), channel_id=1, replica_groups=mesh['tok'=4,'col_0'=8,'col_1'=4,'col_2'=2] {'col_0','col_1','col_2'}, dimensions={0} | all-to-all | bytes 393216 | tf_op jit(solution)/shard_map/all_to_all | solution.py:28
  43.1 4.8 %all-to-all-start.1 = ((bf16[64,12,128]{2,1,0:T(8,128)(2,1)}), bf16[64,12,128]{2,1,0:T(8,128)(2,1)S(1)}, u32[]{:S(2)}, u32[]{:S(2)}) async-start(bf16[64,12,128]{2,1,0:T(8,128)(2,1)} %get-tuple-element.8), calls=%async_computation.1 | async-start | bytes 524288 | tf_op jit(solution)/shard_map/all_to_all | solution.py:28
  48.0 0.3 reshape_squeeze.6
  48.3 0.3 copy.9
  48.6 0.5 fusion.11
  49.1 0.4 copy.10
  49.4 0.8 broadcast_in_dim_reshape.6
  50.3 10.7 %all-to-all-done.1 = bf16[64,12,128]{2,1,0:T(8,128)(2,1)S(1)} async-done(((bf16[64,12,128]{2,1,0:T(8,128)(2,1)}), bf16[64,12,128]{2,1,0:T(8,128)(2,1)S(1)}, u32[]{:S(2)}, u32[]{:S(2)}) %all-to-all-start.1) | async-done | bytes 196640 | tf_op jit(solution)/shard_map/all_to_all | solution.py:28
  61.0 0.3 reshape_squeeze.7
  61.3 0.3 copy.12
  61.6 0.4 fusion.12
  62.1 0.4 copy.13
  62.5 0.8 broadcast_in_dim_reshape.7
  63.3 1.6 multiply_reduce_fusion
  64.9 0.2 reduce-scatter.2.cloned.1.call-start
  65.1 116.2 %all-gather.2.cloned.1.call-done = bf16[1,1536,8192]{2,1,0:T(8,128)(2,1)} async-done(((bf16[1,24,8192]{2,1,0:T(8,128)(2,1)}), bf16[1,1536,8192]{2,1,0:T(8,128)(2,1)}) %all-gather.2.cloned.1.call-update) | async-done | bytes 25165840 | tf_op jit(solution)/shard_map/all_gather | solution.py:84
  181.4 13.1 %fusion = f32[8192,128]{1,0:T(8,128)} fusion(bf16[1,1536,8192]{2,1,0:T(8,128)(2,1)} %all-gather.2.cloned.1.call-done, s32[]{:T(128)S(6)} %select_n.15), kind=kOutput, calls=%fused_computation.1 | convolution fusion | flops 3221225472 | bytes 29753348 | tf_op jit(solution)/shard_map/dot_general | solution.py:86
  194.4 9.0 %psum.28 = f32[]{:T(128)} all-reduce(f32[]{:T(128)} %get-tuple-element.5), channel_id=1, replica_groups=mesh['tok'=4,'col_0'=8,'col_1'=4,'col_2'=2] {'tok'}, use_global_device_ids=true, to_apply=%region_2.3 | all-reduce | flops 1 | bytes 8 | tf_op jit(solution)/shard_map/psum | solution.py:38
  203.4 14.0 %psum.29 = f32[]{:T(128)} all-reduce(f32[]{:T(128)} %psum.28), channel_id=1, replica_groups=mesh['tok'=4,'col_0'=8,'col_1'=4,'col_2'=2] {'col_0'}, use_global_device_ids=true, to_apply=%region_3.4 | all-reduce | flops 1 | bytes 8 | tf_op jit(solution)/shard_map/psum | solution.py:38
  217.4 7.6 %psum.30 = f32[]{:T(128)} all-reduce(f32[]{:T(128)} %psum.29), channel_id=1, replica_groups=mesh['tok'=4,'col_0'=8,'col_1'=4,'col_2'=2] {'col_1'}, use_global_device_ids=true, to_apply=%region_4.5 | all-reduce | flops 1 | bytes 8 | tf_op jit(solution)/shard_map/psum | solution.py:38
  225.7 8.8 %psum.31 = f32[]{:T(128)} all-reduce(f32[]{:T(128)} %psum.30), channel_id=1, replica_groups=mesh['tok'=4,'col_0'=8,'col_1'=4,'col_2'=2] {'col_2'}, use_global_device_ids=true, to_apply=%region_5.6 | all-reduce | flops 1 | bytes 8 | tf_op jit(solution)/shard_map/psum | solution.py:38
  235.2 5.4 %reduce-scatter.2.cloned.1.call-done = f32[2048,128]{1,0:T(8,128)} async-done(((f32[8192,128]{1,0:T(8,128)}), f32[2048,128]{1,0:T(8,128)}) %reduce-scatter.2.cloned.1.call-update) | async-done | bytes 1048592 | tf_op jit(solution)/shard_map/reduce_scatter | solution.py:89
  240.5 2.5 %select_add_fusion = f32[2048,128]{1,0:T(8,128)} fusion(f32[2048,128]{1,0:T(8,128)} %reduce-scatter.2.cloned.1.call-done, f32[]{:T(128)S(6)} %mul.59, s32[128]{0:T(128)S(1)} %iota_add_fusion.1, s32[2048]{0:T(1024)S(1)} %iota_add_fusion), kind=kLoop, calls=%fused_computation.4 | loop fusion | flops 1048576 | bytes 2105860 | tf_op jit(solution)/shard_map/add | solution.py:96
  (11 shorter events, 0.4 us)
Async XLA Ops:
  43.1 17.9 %all-to-all-start.1 = ((bf16[64,12,128]{2,1,0:T(8,128)(2,1)}), bf16[64,12,128]{2,1,0:T(8,128)(2,1)S(1)}, u32[]{:S(2)}, u32[]{:S(2)}) async-start(bf16[64,12,128]{2,1,0:T(8,128)(2,1)} %get-tuple-element.8), calls=%async_computation.1 | async-start | bytes 524288 | tf_op jit(solution)/shard_map/all_to_all | solution.py:28
  47.9 133.5 %all-gather.2.cloned.1.call-start = ((), (), s32[]{:S(2)}) async-start(), calls=%async_computation.3 | async-start | bytes 25559040 | tf_op jit(solution)/shard_map/all_gather | solution.py:84
  64.9 175.7 %reduce-scatter.2.cloned.1.call-start = ((), (), s32[]{:S(2)}) async-start(), calls=%async_computation.4 | async-start | bytes 5242880 | tf_op jit(solution)/shard_map/reduce_scatter | solution.py:89
Sparse Core Ops, SparseCore 0:
  65.0 116.3 all-gather.1
  194.6 45.9 reduce-scatter.1
where the time goes:
time: 250 us
  waiting for transfers between devices  132 us (53%)
  blocking collectives  65.2 us (26%)
  between operations  14.9 us (6%)
  matrix products  14.3 us (6%)
  local copies, waits for them, and re-layouts  12 us (5%)
  other arithmetic  6.24 us (2%)
  starting transfers between devices  5.04 us (2%)
    all_gather x1, waiting for transfers between devices, shards(): flat = lax.all_gather(finished, COL, axis=1, tiled=True).reshape(-1, D)  116 us
    psum x4, blocking collectives, by_axis(): x = lax.psum(x, axis)  39.3 us
    all_to_all x1, blocking collectives, grouped_exchange(): lax.all_to_all(group, axis, split_axis=split_dim, concat_axis=concat_dim,...  25.8 us
    dot_general x1, matrix products, shards(): lax.dot_general(flat, own_cols, (((0,), (0,)), ((), ())), preferred_eleme...  13.1 us
    all_to_all x1, waiting for transfers between devices, grouped_exchange(): lax.all_to_all(group, axis, split_axis=split_dim, concat_axis=concat_dim,...  10.7 us
    gather x2, local copies, waits for them, and re-layouts, shards(): jnp.take(row_bank, token_ids, axis=0)  5.55 us
    reduce_scatter x1, waiting for transfers between devices, shards(): lax.psum_scatter(partial_sum, 'tok', scatter_dimension=0, tiled=True)  5.38 us
  transfers between devices with their start and end apart: 3, of which 3 were waited for; matrix products, arithmetic and copies ran while one was open for 1% of the time, Pallas kernels for 0%

commit v1 on v0

v1 whole, which is shorter than its diff:
```python
import functools
import math

import jax
import jax.numpy as jnp
import numpy as np
from jax import lax
from jax.experimental import pallas as pl
from jax.experimental.pallas import tpu as pltpu
from jax.sharding import Mesh
from jax.sharding import PartitionSpec as P

D = 8192
BLOCK = 32
TOKENS = 6144
COL = ("z", "x", "c")
NY, NZ, NX, NC = 4, 8, 4, 2
TG = TOKENS // (NY * NX)
MESH = pl.DeviceIdType.MESH
NT = (((1,), (1,)), ((), ()))
NN = (((1,), (0,)), ((), ()))


def parity_sign(v):
    v = v ^ (v >> 4)
    v = v ^ (v >> 2)
    v = v ^ (v >> 1)
    return 1 - 2 * (v & 1)


def inner_table():
    r = np.arange(128)
    b_r, a_r = (r >> 4) * 4 + (r & 3), (r >> 2) & 3
    b_c, a_c = r & 31, r >> 5
    bits = np.array([bin(i).count("1") & 1 for i in range(32)])
    signs = 1 - 2 * bits[b_r[:, None] & b_c[None, :]]
    return np.where(a_r[:, None] == a_c[None, :], signs, 0).astype(np.float32)


def outer_table(core, for_rows):
    r = lax.broadcasted_iota(jnp.int32, (512, 1), 0)
    k = lax.broadcasted_iota(jnp.int32, (1, 1024), 1)
    if for_rows:
        c = ((r >> 7) << 6) | ((r & 7) << 3) | ((r >> 5) & 3)
        b_r = (r >> 3) & 3
    else:
        c = ((r >> 6) << 5) | (((r >> 4) & 3) << 3) | ((r >> 2) & 3)
        b_r = r & 3
    c = c | (core << 2)
    a = (((k >> 6) & 7) << 5) | (((k >> 4) & 3) << 3) | ((k >> 9) << 2) | ((k >> 2) & 3)
    sign = parity_sign(c & a)
    return jnp.where(b_r == (k & 3), sign, 0).astype(jnp.float32).astype(jnp.bfloat16)


def column_order():
    o = lax.broadcasted_iota(jnp.int32, (128, 128), 0)
    i = lax.broadcasted_iota(jnp.int32, (128, 128), 1)
    src = (((o >> 2) & 7) << 4) | ((o >> 5) << 2) | (o & 3)
    return (i == src).astype(jnp.float32).astype(jnp.bfloat16)


def kernel(
    picked, hs, out, tr,
    hb, x1, x2, hm, hn, rm, rn, mb, nz, np_, g, ra, rb, ts, trx,
    s1, r1, s2, r2, s3, r3, sn, rn_sem, sm, rm_sem, sy, ry, sr, rr, sl, rl, sd, rd,
    sa, ra_sem, sb, rb_sem, st, rt,
):
    y, z, x, c = (lax.axis_index(n) for n in ("tok", "z", "x", "c"))
    scale = 1.0 / math.sqrt(D)

    def at_x(d):
        return lax.rem(x + d + NX, NX)

    def at_y(d):
        return lax.rem(y + d + NY, NY)

    def at_z(d):
        return lax.rem(z + d + NZ, NZ)

    def copy(src, dst, send, recv, **where):
        return pltpu.make_async_remote_copy(
            src_ref=src, dst_ref=dst, send_sem=send, recv_sem=recv,
            device_id=where, device_id_type=MESH,
        )

    started = []

    def send(*args, **where):
        cp = copy(*args, **where)
        cp.start()
        started.append(cp)

    def arrived(ref, sem):
        copy(ref, ref, sem, sem, c=1 - c).wait_recv()

    barrier = pltpu.get_barrier_semaphore()
    peers = (
        [dict(x=at_x(d)) for d in range(1, NX)]
        + [dict(tok=at_y(d)) for d in range(1, NY)]
        + [dict(z=at_z(d)) for d in range(1, NZ)]
        + [dict(c=1 - c)]
    )
    for where in peers:
        pl.semaphore_signal(barrier, inc=1, device_id=where, device_id_type=MESH)

    for j in range(NX):
        h = lax.dot_general(
            hs[...], picked[j * TG : (j + 1) * TG, :], NT, preferred_element_type=jnp.float32
        )
        hb[j] = h.astype(jnp.bfloat16)
    x1[x] = hb[x]
    pl.semaphore_wait(barrier, len(peers))

    for d in range(1, NX):
        send(hb.at[at_x(d)], x1.at[x], s1.at[d - 1], r1.at[d - 1], x=at_x(d))
    hn[...] = outer_table(c, False)
    for d in range(1, NX):
        arrived(x1.at[at_x(-d)], r1.at[d - 1])

    def piece(zz):
        return x1.at[:, pl.ds(pl.multiple_of(zz * 16, 16), 16), :]

    for d in range(1, NZ):
        send(piece(at_z(d)), x2.at[c, z], s2.at[d - 1], r2.at[d - 1], z=at_z(d))
    send(piece(z), x2.at[c, z], s3.at[0], r3.at[0], c=1 - c)
    x2[c, z] = x1[:, pl.ds(pl.multiple_of(z * 16, 16), 16), :]
    hm[...] = outer_table(c, True)
    for d in range(1, NZ):
        got = x2.at[c, at_z(-d)]
        arrived(got, r2.at[d - 1])
        send(got, got, s3.at[d], r3.at[d], c=1 - c)
    for d in range(NZ):
        arrived(x2.at[1 - c, at_z(-d)], r3.at[d])

    spread = x2[...].reshape(1024, TG)

    def turn(table):
        return (
            lax.dot_general(table[...], spread, NN, preferred_element_type=jnp.float32) * scale
        ).astype(jnp.bfloat16)

    rn[...] = turn(hn).reshape(NZ, 64, TG)
    for d in range(1, NZ):
        send(rn.at[at_z(d)], nz.at[z, y], sn.at[d - 1], rn_sem.at[d - 1], z=at_z(d))
    nz[z, y] = rn[z]
    rows = turn(hm)
    rm[...] = rows.reshape(NY, 128, TG)
    for d in range(1, NY):
        send(rm.at[at_y(d)], mb.at[z, c, y], sm.at[d - 1], rm_sem.at[d - 1], tok=at_y(d))
    mb[z, c, y] = rm[y]

    def share_columns(d):
        got = nz.at[at_z(-d), y]
        for e in range(1, NY):
            send(got, got, sy.at[d, e - 1], ry.at[d, e - 1], tok=at_y(e))

    share_columns(0)

    sq = rows.astype(jnp.float32)
    sq = jnp.sum((sq * sq).reshape(64, 8, TG), axis=0)
    sq = sq[:, :128] + sq[:, 128:256] + sq[:, 256:]

    stages = [
        [dict(c=1 - c)],
        [dict(x=at_x(d)) for d in range(1, NX)],
        [dict(tok=at_y(d)) for d in range(1, NY)],
        [dict(z=at_z(d)) for d in range(1, NZ)],
    ]
    base = [0, 1, 4, 7]

    def trace_send(k):
        for i, where in enumerate(stages[k]):
            j = base[k] + i
            send(ts.at[k], trx.at[j], st.at[j], rt.at[j], **where)

    def trace_take(k):
        total = ts[k]
        for i in range(len(stages[k])):
            j = base[k] + i
            arrived(trx.at[j], rt.at[j])
            total = total + trx[j]
        return total

    ts[0] = sq
    trace_send(0)

    for d in range(1, NY):
        arrived(mb.at[z, c, at_y(-d)], rm_sem.at[d - 1])

    def ring(slot, s):
        if s < 4:
            send(mb.at[slot[0], c], mb.at[slot[0], c], sr.at[s - 1], rr.at[s - 1], z=at_z(1))
            send(mb.at[slot[1], c], mb.at[slot[1], c], sl.at[s - 1], rl.at[s - 1], z=at_z(-1))
        else:
            a, b = mb.at[slot[0], c, 0:2], mb.at[slot[1], c, 2:4]
            send(a, a, sr.at[s - 1], rr.at[s - 1], z=at_z(1))
            send(b, b, sl.at[s - 1], rl.at[s - 1], z=at_z(-1))

    def share(slot, k):
        got = mb.at[slot, c]
        send(got, got, sd.at[k], rd.at[k], c=1 - c)

    ring((z, z), 1)
    share(z, 0)

    for d in range(1, NZ):
        arrived(nz.at[at_z(-d), y], rn_sem.at[d - 1])
        share_columns(d)

    def ring_take(s):
        if s < 4:
            arrived(mb.at[at_z(-s), c], rr.at[s - 1])
            arrived(mb.at[at_z(s), c], rl.at[s - 1])
            ring((at_z(-s), at_z(s)), s + 1)
            share(at_z(-s), 2 * s - 1)
            share(at_z(s), 2 * s)
        else:
            arrived(mb.at[at_z(4), c, 0:2], rr.at[3])
            arrived(mb.at[at_z(4), c, 2:4], rl.at[3])
            share(at_z(4), 7)

    ring_take(1)
    ts[1] = trace_take(0)
    trace_send(1)

    order = column_order()
    for d in range(NZ):
        for e in range(1, NY):
            arrived(nz.at[at_z(-d), at_y(-e)], ry.at[d, e - 1])
    for j in range(NX):
        for e in range(NY):
            part = nz[:, e, j * 16 : (j + 1) * 16, :].reshape(128, TG)
            np_[j * 128 : (j + 1) * 128, e * TG : (e + 1) * TG] = lax.dot_general(
                order, part, NN, preferred_element_type=jnp.float32
            ).astype(jnp.bfloat16)

    slots = [z, at_z(-1), at_z(1), at_z(-2), at_z(2), at_z(-3), at_z(3), at_z(4)]
    right, left = at_x(1), at_x(-1)

    def multiply(k):
        slot = slots[k]
        arrived(mb.at[slot, 1 - c], rd.at[k])
        lhs = jnp.concatenate(
            [
                jnp.concatenate([mb[slot, e, f] for f in range(NY)], axis=1)
                for e in range(NC)
            ],
            axis=0,
        )
        prod = lax.dot_general(lhs, np_[...], NT, preferred_element_type=jnp.float32)
        for j in range(NX):
            g[k, j] = prod[:, j * 128 : (j + 1) * 128]
        far = g.at[k, at_x(2)]
        send(far.at[0:128], ra.at[k, 0], sa.at[k, 0], ra_sem.at[k, 0], x=right)
        send(far.at[128:256], ra.at[k, 1], sa.at[k, 1], ra_sem.at[k, 1], x=left)

    def pass_on(k):
        arrived(ra.at[k, 0], ra_sem.at[k, 0])
        g[k, right, 0:128, :] = g[k, right, 0:128, :] + ra[k, 0]
        send(g.at[k, right], rb.at[k, 0], sb.at[k, 0], rb_sem.at[k, 0], x=right)
        arrived(ra.at[k, 1], ra_sem.at[k, 1])
        g[k, left, 128:256, :] = g[k, left, 128:256, :] + ra[k, 1]
        send(g.at[k, left], rb.at[k, 1], sb.at[k, 1], rb_sem.at[k, 1], x=left)

    def finish(k):
        arrived(rb.at[k, 0], rb_sem.at[k, 0])
        arrived(rb.at[k, 1], rb_sem.at[k, 1])
        total = g[k, x] + rb[k, 0] + rb[k, 1]
        for i in range(32):
            start = (i >> 2) * 32 + (i & 3) + slots[k] * 4
            out[pl.ds(start, 8, stride=256), :] = total[i * 8 : (i + 1) * 8, :]

    multiply(0)
    multiply(1)
    pass_on(0)
    multiply(2)
    pass_on(1)
    ring_take(2)
    ts[2] = trace_take(1)
    trace_send(2)
    finish(0)
    multiply(3)
    pass_on(2)
    finish(1)
    multiply(4)
    pass_on(3)
    finish(2)
    ring_take(3)
    ts[3] = trace_take(2)
    trace_send(3)
    multiply(5)
    pass_on(4)
    finish(3)
    multiply(6)
    pass_on(5)
    finish(4)
    ring_take(4)
    multiply(7)
    pass_on(6)
    finish(5)
    tr[...] = trace_take(3)
    pass_on(7)
    finish(6)
    finish(7)
    for cp in started:
        cp.wait_send()


def rotate_and_multiply(picked, hs):
    bf, f32 = jnp.bfloat16, jnp.float32
    V = pltpu.VMEM
    dma = pltpu.SemaphoreType.DMA
    scratch = [
        V((NX, 128, TG), bf),
        V((NX, 128, TG), bf),
        V((NC, NZ, NX, 16, TG), bf),
        V((512, 1024), bf),
        V((512, 1024), bf),
        V((NY, 128, TG), bf),
        V((NZ, 64, TG), bf),
        V((NZ, NC, NY, 128, TG), bf),
        V((NZ, NY, 64, TG), bf),
        V((512, NY * TG), bf),
        V((NZ, NX, 256, 128), f32),
        V((NZ, 2, 128, 128), f32),
        V((NZ, 2, 256, 128), f32),
        V((4, 8, 128), f32),
        V((14, 8, 128), f32),
        dma((3,)), dma((3,)), dma((7,)), dma((7,)), dma((8,)), dma((8,)),
        dma((7,)), dma((7,)), dma((3,)), dma((3,)), dma((8, 3)), dma((8, 3)),
        dma((4,)), dma((4,)), dma((4,)), dma((4,)), dma((8,)), dma((8,)),
        dma((8, 2)), dma((8, 2)), dma((8, 2)), dma((8, 2)), dma((14,)), dma((14,)),
    ]
    vmem = pl.BlockSpec(memory_space=pltpu.VMEM)
    return pl.pallas_call(
        kernel,
        out_shape=(
            jax.ShapeDtypeStruct((2048, 128), f32),
            jax.ShapeDtypeStruct((8, 128), f32),
        ),
        in_specs=[vmem, vmem],
        out_specs=(vmem, vmem),
        scratch_shapes=scratch,
        compiler_params=pltpu.CompilerParams(
            collective_id=0, has_side_effects=True, vmem_limit_bytes=48 * 1024 * 1024
        ),
    )(picked, hs)


def shards(row_bank, token_ids, sign_flips, damping):
    picked = row_bank.at[token_ids].get(mode="promise_in_bounds")
    hs = (jnp.asarray(inner_table()) * sign_flips.astype(jnp.float32)[None, :]).astype(
        jnp.bfloat16
    )
    gram, squares = rotate_and_multiply(picked, hs)
    mean_diag = jnp.sum(squares) / TOKENS / D
    row_index = lax.axis_index("tok") * 2048 + lax.broadcasted_iota(jnp.int32, gram.shape, 0)
    col_index = lax.axis_index(COL) * 128 + lax.broadcasted_iota(jnp.int32, gram.shape, 1)
    on_diag = (row_index == col_index).astype(jnp.float32)
    return gram / TOKENS + damping[0] * mean_diag * on_diag


def solution(mesh):
    split = Mesh(mesh.devices.reshape(NY, NZ, NX, NC), ("tok",) + COL)
    return jax.shard_map(
        shards,
        mesh=split,
        in_specs=(P(None, COL), P("tok"), P(COL), P()),
        out_specs=P("tok", COL),
        check_vma=False,
    )
```

time: 250 us -> 105 us (0.42)
  waiting for transfers between devices: 132 us -> 0 us
  Pallas kernels: 0 us -> 93.7 us
  blocking collectives: 65.2 us -> 0 us
  matrix products: 14.3 us -> 0 us
  between operations: 14.9 us -> 1.38 us
  local copies, waits for them, and re-layouts: 12 us -> 5.36 us
  starting transfers between devices: 5.04 us -> 0 us
    all_gather x1 -> x0, waiting for transfers between devices: 116 us -> none  [shards(): flat = lax.all_gather(finished, COL, axis=1, tiled=True).reshape(-1, D)]
    pallas_call x0 -> x1, Pallas kernels: none -> 93.7 us  [rotate_and_multiply(): pl.pallas_call(kernel, out_shape=(jax.ShapeDtypeStruct((2048, 128), f32),...]
    psum x4 -> x0, blocking collectives: 39.3 us -> none  [by_axis(): x = lax.psum(x, axis)]
    all_to_all x1 -> x0, blocking collectives: 25.8 us -> none  [grouped_exchange(): lax.all_to_all(group, axis, split_axis=split_dim, concat_axis=concat_dim,...]
    dot_general x2 -> x0, matrix products: 13.4 us -> none  [the longest x1 13.1 us: shards(): lax.dot_general(flat, own_cols, (((0,), (0,)), ((), ())), preferred_eleme...]
    all_to_all x1 -> x0, waiting for transfers between devices: 10.7 us -> none  [grouped_exchange(): lax.all_to_all(group, axis, split_axis=split_dim, concat_axis=concat_dim,...]
    reduce_scatter x1 -> x0, waiting for transfers between devices: 5.38 us -> none  [shards(): lax.psum_scatter(partial_sum, 'tok', scatter_dimension=0, tiled=True)]
    all_to_all x1 -> x0, starting transfers between devices: 4.77 us -> none  [grouped_exchange(): lax.all_to_all(group, axis, split_axis=split_dim, concat_axis=concat_dim,...]
  transfers between devices with their start and end apart: 3 -> 0, of which waited for: 3 -> 0; matrix products, arithmetic and copies ran while one was open for 1% -> 0% of each run, Pallas kernels for 0% -> 0%
where the time goes in v1:
time: 105 us
  Pallas kernels  93.7 us (89%)
  local copies, waits for them, and re-layouts  5.36 us (5%)
  other arithmetic  4.21 us (4%)
  between operations  1.38 us (1%)
    pallas_call x1, Pallas kernels, rotate_and_multiply(): pl.pallas_call(kernel, out_shape=(jax.ShapeDtypeStruct((2048, 128), f32),...  93.7 us
    gather x1, local copies, waits for them, and re-layouts, shards(): picked = row_bank.at[token_ids].get(mode='promise_in_bounds')  5.36 us

profile of v1, /device:TPU:1, one launch (start us, length us, event | category | flops | bytes accessed | tf_op | source)
XLA Modules:
  0.0 104.7 jit_solution(8558637084763877259)
XLA Ops:
  0.7 0.7 convert_element_type.7
  1.3 0.7 compare_select_fusion
  2.0 0.8 multiply_convert_fusion.hs
  2.9 5.4 %gather_fusion = bf16[1536,128]{1,0:T(8,128)(2,1)S(1)} fusion(bf16[16384,128]{1,0:T(8,128)(2,1)} %param.5, s32[2048]{0:T(1024)S(1)} %pad_clamp_fusion), kind=kCustom, calls=%fused_computation | custom fusion | bytes 792576 | tf_op jit(solution)/shard_map/gather | solution.py:351
  8.3 93.7 %shard_map.55 = (f32[2048,128]{1,0:T(8,128)S(1)}, f32[8,128]{1,0:T(8,128)S(1)}) custom-call(bf16[1536,128]{1,0:T(8,128)(2,1)S(1)} %gather_fusion, bf16[128,128]{1,0:T(8,128)(2,1)S(1)} %multiply_convert_fusion.hs), custom_call_target="tpu_custom_call" | custom-call | tf_op jit(solution)/shard_map/pallas_call | solution.py:335
  102.0 0.7 reduce_sum.9
  103.4 1.3 %select_add_fusion = f32[2048,128]{1,0:T(8,128)} fusion(f32[2048,128]{1,0:T(8,128)S(1)} %get-tuple-element.7, f32[]{:T(128)S(6)} %mul.35, s32[128]{0:T(128)S(1)} %iota_add_fusion.1, s32[2048]{0:T(1024)S(1)} %iota_add_fusion), kind=kLoop, calls=%fused_computation.1 | loop fusion | flops 1048576 | bytes 2105860 | tf_op jit(solution)/shard_map/add | solution.py:360
  (3 shorter events, 0.0 us)

commit v2 on v1

--- a/solution.py
+++ b/solution.py
@@ -16,6 +16,9 @@
 COL = ("z", "x", "c")
 NY, NZ, NX, NC = 4, 8, 4, 2
 TG = TOKENS // (NY * NX)
+TT = 128
+NT3 = TG // TT
+HOPS = (4, 1, 7, 2, 6, 3, 5)
 MESH = pl.DeviceIdType.MESH
 NT = (((1,), (1,)), ((), ()))
 NN = (((1,), (0,)), ((), ()))
@@ -60,7 +63,7 @@
 
 
 def kernel(
-    picked, hs, out, tr,
+    picked, hs, signs, out, tr,
     hb, x1, x2, hm, hn, rm, rn, mb, nz, np_, g, ra, rb, ts, trx,
     s1, r1, s2, r2, s3, r3, sn, rn_sem, sm, rm_sem, sy, ry, sr, rr, sl, rl, sd, rd,
     sa, ra_sem, sb, rb_sem, st, rt,
@@ -103,62 +106,79 @@
     for where in peers:
         pl.semaphore_signal(barrier, inc=1, device_id=where, device_id_type=MESH)
 
-    for j in range(NX):
-        h = lax.dot_general(
-            hs[...], picked[j * TG : (j + 1) * TG, :], NT, preferred_element_type=jnp.float32
-        )
-        hb[j] = h.astype(jnp.bfloat16)
-    x1[x] = hb[x]
-    pl.semaphore_wait(barrier, len(peers))
-
-    for d in range(1, NX):
-        send(hb.at[at_x(d)], x1.at[x], s1.at[d - 1], r1.at[d - 1], x=at_x(d))
+    signed = (hs[...] * signs[...].astype(jnp.float32)).astype(jnp.bfloat16)
+    for t in range(NT3):
+        for j in range(NX):
+            first = j * TG + t * TT
+            h = lax.dot_general(
+                signed, picked[first : first + TT, :], NT, preferred_element_type=jnp.float32
+            )
+            hb[t, j] = h.astype(jnp.bfloat16)
+        if t == 0:
+            pl.semaphore_wait(barrier, len(peers))
+        for d in range(1, NX):
+            send(hb.at[t, at_x(d)], x1.at[t, x], s1.at[t, d - 1], r1.at[t, d - 1], x=at_x(d))
+        x1[t, x] = hb[t, x]
     hn[...] = outer_table(c, False)
-    for d in range(1, NX):
-        arrived(x1.at[at_x(-d)], r1.at[d - 1])
-
-    def piece(zz):
-        return x1.at[:, pl.ds(pl.multiple_of(zz * 16, 16), 16), :]
-
-    for d in range(1, NZ):
-        send(piece(at_z(d)), x2.at[c, z], s2.at[d - 1], r2.at[d - 1], z=at_z(d))
-    send(piece(z), x2.at[c, z], s3.at[0], r3.at[0], c=1 - c)
-    x2[c, z] = x1[:, pl.ds(pl.multiple_of(z * 16, 16), 16), :]
+
+    def piece(t, zz):
+        return x1.at[t, :, pl.ds(pl.multiple_of(zz * 16, 16), 16), :]
+
+    for t in range(NT3):
+        for d in range(1, NX):
+            arrived(x1.at[t, at_x(-d)], r1.at[t, d - 1])
+        for d in HOPS:
+            send(piece(t, at_z(d)), x2.at[t, c, z], s2.at[t, d - 1], r2.at[t, d - 1], z=at_z(d))
+        send(piece(t, z), x2.at[t, c, z], s3.at[t, 0], r3.at[t, 0], c=1 - c)
+        x2[t, c, z] = x1[t, :, pl.ds(pl.multiple_of(z * 16, 16), 16), :]
     hm[...] = outer_table(c, True)
-    for d in range(1, NZ):
-        got = x2.at[c, at_z(-d)]
-        arrived(got, r2.at[d - 1])
-        send(got, got, s3.at[d], r3.at[d], c=1 - c)
-    for d in range(NZ):
-        arrived(x2.at[1 - c, at_z(-d)], r3.at[d])
-
-    spread = x2[...].reshape(1024, TG)
-
-    def turn(table):
-        return (
-            lax.dot_general(table[...], spread, NN, preferred_element_type=jnp.float32) * scale
-        ).astype(jnp.bfloat16)
-
-    rn[...] = turn(hn).reshape(NZ, 64, TG)
-    for d in range(1, NZ):
-        send(rn.at[at_z(d)], nz.at[z, y], sn.at[d - 1], rn_sem.at[d - 1], z=at_z(d))
-    nz[z, y] = rn[z]
-    rows = turn(hm)
-    rm[...] = rows.reshape(NY, 128, TG)
-    for d in range(1, NY):
-        send(rm.at[at_y(d)], mb.at[z, c, y], sm.at[d - 1], rm_sem.at[d - 1], tok=at_y(d))
-    mb[z, c, y] = rm[y]
-
-    def share_columns(d):
-        got = nz.at[at_z(-d), y]
-        for e in range(1, NY):
-            send(got, got, sy.at[d, e - 1], ry.at[d, e - 1], tok=at_y(e))
-
-    share_columns(0)
-
-    sq = rows.astype(jnp.float32)
-    sq = jnp.sum((sq * sq).reshape(64, 8, TG), axis=0)
-    sq = sq[:, :128] + sq[:, 128:256] + sq[:, 256:]
+
+    def share_turned(t):
+        for d in HOPS:
+            got = x2.at[t, c, at_z(-d)]
+            arrived(got, r2.at[t, d - 1])
+            send(got, got, s3.at[t, d], r3.at[t, d], c=1 - c)
+
+    def turn(t):
+        for d in range(NZ):
+            arrived(x2.at[t, 1 - c, at_z(-d)], r3.at[t, d])
+        spread = x2[t].reshape(1024, TT)
+
+        def times(table):
+            return (
+                lax.dot_general(table[...], spread, NN, preferred_element_type=jnp.float32) * scale
+            ).astype(jnp.bfloat16)
+
+        rn[t] = times(hn).reshape(NZ, 64, TT)
+        for d in HOPS:
+            send(
+                rn.at[t, at_z(d)], nz.at[z, y, t], sn.at[t, d - 1], rn_sem.at[t, d - 1], z=at_z(d)
+            )
+        nz[z, y, t] = rn[t, z]
+        rows = times(hm)
+        rm[t] = rows.reshape(NY, 128, TT)
+        for d in range(1, NY):
+            send(
+                rm.at[t, at_y(d)], mb.at[z, c, y, t], sm.at[t, d - 1], rm_sem.at[t, d - 1],
+                tok=at_y(d),
+            )
+        mb[z, c, y, t] = rm[t, y]
+        sq = rows.astype(jnp.float32)
+        return jnp.sum((sq * sq).reshape(64, 8, TT), axis=0)
+
+    def near(t, d):
+        got = nz.at[at_z(-d), y, t]
+        send(got, got, sy.at[t, d, 0], ry.at[t, d, 0], tok=at_y(1))
+        send(got, got, sy.at[t, d, 1], ry.at[t, d, 1], tok=at_y(-1))
+
+    def far(t, d):
+        left, right = nz.at[at_z(-d), at_y(-1), t], nz.at[at_z(-d), at_y(1), t]
+        arrived(left, ry.at[t, d, 0])
+        arrived(right, ry.at[t, d, 1])
+        if (t + d) % 2 == 0:
+            send(left, left, sy.at[t, d, 2], ry.at[t, d, 2], tok=at_y(1))
+        else:
+            send(right, right, sy.at[t, d, 2], ry.at[t, d, 2], tok=at_y(-1))
 
     stages = [
         [dict(c=1 - c)],
@@ -180,12 +200,6 @@
             arrived(trx.at[j], rt.at[j])
             total = total + trx[j]
         return total
-
-    ts[0] = sq
-    trace_send(0)
-
-    for d in range(1, NY):
-        arrived(mb.at[z, c, at_y(-d)], rm_sem.at[d - 1])
 
     def ring(slot, s):
         if s < 4:
@@ -199,13 +213,6 @@
     def share(slot, k):
         got = mb.at[slot, c]
         send(got, got, sd.at[k], rd.at[k], c=1 - c)
-
-    ring((z, z), 1)
-    share(z, 0)
-
-    for d in range(1, NZ):
-        arrived(nz.at[at_z(-d), y], rn_sem.at[d - 1])
-        share_columns(d)
 
     def ring_take(s):
         if s < 4:
@@ -219,20 +226,47 @@
             arrived(mb.at[at_z(4), c, 2:4], rl.at[3])
             share(at_z(4), 7)
 
-    ring_take(1)
+    share_turned(0)
+    share_turned(1)
+    sq = turn(0)
+    share_turned(2)
+    sq = sq + turn(1)
+    sq = sq + turn(2)
+    ts[0] = sq
+    trace_send(0)
+    for t in range(NT3):
+        near(t, 0)
+        for d in range(1, NY):
+            arrived(mb.at[z, c, at_y(-d), t], rm_sem.at[t, d - 1])
+    ring((z, z), 1)
+    share(z, 0)
+    for t in range(NT3):
+        for d in HOPS:
+            arrived(nz.at[at_z(-d), y, t], rn_sem.at[t, d - 1])
+            near(t, d)
+        if t == 0:
+            for e in range(NT3):
+                far(e, 0)
+        else:
+            for d in HOPS:
+                far(t - 1, d)
+    for d in HOPS:
+        far(NT3 - 1, d)
     ts[1] = trace_take(0)
     trace_send(1)
 
     order = column_order()
-    for d in range(NZ):
-        for e in range(1, NY):
-            arrived(nz.at[at_z(-d), at_y(-e)], ry.at[d, e - 1])
-    for j in range(NX):
+    for t in range(NT3):
+        for d in range(NZ):
+            arrived(nz.at[at_z(-d), at_y(2), t], ry.at[t, d, 2])
         for e in range(NY):
-            part = nz[:, e, j * 16 : (j + 1) * 16, :].reshape(128, TG)
-            np_[j * 128 : (j + 1) * 128, e * TG : (e + 1) * TG] = lax.dot_general(
-                order, part, NN, preferred_element_type=jnp.float32
-            ).astype(jnp.bfloat16)
+            lane = e * TG + t * TT
+            for j in range(NX):
+                part = nz[:, e, t, j * 16 : (j + 1) * 16, :].reshape(128, TT)
+                np_[j * 128 : (j + 1) * 128, lane : lane + TT] = lax.dot_general(
+                    order, part, NN, preferred_element_type=jnp.float32
+                ).astype(jnp.bfloat16)
+    ring_take(1)
 
     slots = [z, at_z(-1), at_z(1), at_z(-2), at_z(2), at_z(-3), at_z(3), at_z(4)]
     right, left = at_x(1), at_x(-1)
@@ -242,7 +276,9 @@
         arrived(mb.at[slot, 1 - c], rd.at[k])
         lhs = jnp.concatenate(
             [
-                jnp.concatenate([mb[slot, e, f] for f in range(NY)], axis=1)
+                jnp.concatenate(
+                    [mb[slot, e, f, t] for f in range(NY) for t in range(NT3)], axis=1
+                )
                 for e in range(NC)
             ],
             axis=0,
@@ -298,7 +334,7 @@
     multiply(7)
     pass_on(6)
     finish(5)
-    tr[...] = trace_take(3)
+    tr[...] = jnp.full((8, 128), jnp.sum(trace_take(3)), jnp.float32)
     pass_on(7)
     finish(6)
     finish(7)
@@ -306,30 +342,33 @@
         cp.wait_send()
 
 
-def rotate_and_multiply(picked, hs):
+def rotate_and_multiply(picked, hs, signs):
     bf, f32 = jnp.bfloat16, jnp.float32
     V = pltpu.VMEM
     dma = pltpu.SemaphoreType.DMA
     scratch = [
-        V((NX, 128, TG), bf),
-        V((NX, 128, TG), bf),
-        V((NC, NZ, NX, 16, TG), bf),
+        V((NT3, NX, 128, TT), bf),
+        V((NT3, NX, 128, TT), bf),
+        V((NT3, NC, NZ, NX, 16, TT), bf),
         V((512, 1024), bf),
         V((512, 1024), bf),
-        V((NY, 128, TG), bf),
-        V((NZ, 64, TG), bf),
-        V((NZ, NC, NY, 128, TG), bf),
-        V((NZ, NY, 64, TG), bf),
+        V((NT3, NY, 128, TT), bf),
+        V((NT3, NZ, 64, TT), bf),
+        V((NZ, NC, NY, NT3, 128, TT), bf),
+        V((NZ, NY, NT3, 64, TT), bf),
         V((512, NY * TG), bf),
         V((NZ, NX, 256, 128), f32),
         V((NZ, 2, 128, 128), f32),
         V((NZ, 2, 256, 128), f32),
         V((4, 8, 128), f32),
         V((14, 8, 128), f32),
-        dma((3,)), dma((3,)), dma((7,)), dma((7,)), dma((8,)), dma((8,)),
-        dma((7,)), dma((7,)), dma((3,)), dma((3,)), dma((8, 3)), dma((8, 3)),
-        dma((4,)), dma((4,)), dma((4,)), dma((4,)), dma((8,)), dma((8,)),
-        dma((8, 2)), dma((8, 2)), dma((8, 2)), dma((8, 2)), dma((14,)), dma((14,)),
+    ] + [
+        dma(shape)
+        for shape in (
+            (NT3, 3), (NT3, 7), (NT3, 8), (NT3, 7), (NT3, 3), (NT3, 8, 3),
+            (4,), (4,), (8,), (8, 2), (8, 2), (14,),
+        )
+        for _ in range(2)
     ]
     vmem = pl.BlockSpec(memory_space=pltpu.VMEM)
     return pl.pallas_call(
@@ -338,22 +377,25 @@
             jax.ShapeDtypeStruct((2048, 128), f32),
             jax.ShapeDtypeStruct((8, 128), f32),
         ),
-        in_specs=[vmem, vmem],
+        in_specs=[vmem, vmem, vmem],
         out_specs=(vmem, vmem),
         scratch_shapes=scratch,
         compiler_params=pltpu.CompilerParams(
             collective_id=0, has_side_effects=True, vmem_limit_bytes=48 * 1024 * 1024
         ),
-    )(picked, hs)
+    )(picked, hs, signs)
 
 
 def shards(row_bank, token_ids, sign_flips, damping):
-    picked = row_bank.at[token_ids].get(mode="promise_in_bounds")
-    hs = (jnp.asarray(inner_table()) * sign_flips.astype(jnp.float32)[None, :]).astype(
-        jnp.bfloat16
+    picked = lax.gather(
+        row_bank,
+        token_ids[:, None],
+        lax.GatherDimensionNumbers((1,), (0,), (0,)),
+        (1, row_bank.shape[1]),
+        mode=lax.GatherScatterMode.PROMISE_IN_BOUNDS,
     )
-    gram, squares = rotate_and_multiply(picked, hs)
-    mean_diag = jnp.sum(squares) / TOKENS / D
+    gram, squares = rotate_and_multiply(picked, jnp.asarray(inner_table()), sign_flips[None, :])
+    mean_diag = squares[0, 0] / TOKENS / D
     row_index = lax.axis_index("tok") * 2048 + lax.broadcasted_iota(jnp.int32, gram.shape, 0)
     col_index = lax.axis_index(COL) * 128 + lax.broadcasted_iota(jnp.int32, gram.shape, 1)
     on_diag = (row_index == col_index).astype(jnp.float32)

time: 105 us -> 99.1 us (0.944)
  Pallas kernels: 93.7 us -> 88.1 us
  other arithmetic: 4.21 us -> 2.02 us
  local copies, waits for them, and re-layouts: 5.36 us -> 7.43 us
    pallas_call x1, Pallas kernels: 93.7 us -> 88.1 us  [rotate_and_multiply(): pl.pallas_call(kernel, out_shape=(jax.ShapeDtypeStruct((2048, 128), f32),...]
    convert_element_type x2 -> x0, other arithmetic: 1.51 us -> none  [the longest x1 0.85 us: shards(): (jnp.asarray(inner_table()) * sign_flips.astype(jnp.float32)[None, :]).as...]
    unnamed x0 -> x4, local copies, waits for them, and re-layouts: none -> 1.49 us
where the time goes in v2:
time: 99.1 us; the launch traced here: 98.9 us
  Pallas kernels  88.1 us (89%)
  local copies, waits for them, and re-layouts  7.43 us (7%)
  other arithmetic  2.02 us (2%)
  between operations  1.33 us (1%)
    pallas_call x1, Pallas kernels, rotate_and_multiply(): pl.pallas_call(kernel, out_shape=(jax.ShapeDtypeStruct((2048, 128), f32),...  88.1 us
    gather x1, local copies, waits for them, and re-layouts, shards(): lax.gather(row_bank, token_ids[:, None], lax.GatherDimensionNumbers((1,),...  5.36 us

profile of v2, /device:TPU:1, one launch (start us, length us, event | category | flops | bytes accessed | tf_op | source)
XLA Modules:
  0.0 98.9 jit_solution(7035515361513589732)
XLA Ops:
  0.7 0.7 pad_clamp_fusion
  1.4 5.4 %gather_fusion = bf16[1536,128]{1,0:T(8,128)(2,1)S(1)} fusion(bf16[16384,128]{1,0:T(8,128)(2,1)} %param.5, s32[2048]{0:T(1024)S(1)} %pad_clamp_fusion), kind=kCustom, calls=%fused_computation | custom fusion | bytes 792576 | tf_op jit(solution)/shard_map/gather | solution.py:390
  6.7 0.0 copy-start
  6.8 0.8 copy-done
  7.6 0.0 copy-start.1
  7.6 0.7 copy-done.1
  8.2 88.1 %shard_map.55 = (f32[2048,128]{1,0:T(8,128)S(1)}, f32[8,128]{1,0:T(8,128)S(1)}) custom-call(bf16[1536,128]{1,0:T(8,128)(2,1)S(1)} %gather_fusion, f32[128,128]{1,0:T(8,128)S(1)} %copy-done, s32[1,128]{1,0:T(1,128)S(1)} %bitcast.4), custom_call_target="tpu_custom_call" | custom-call | tf_op jit(solution)/shard_map/pallas_call | solution.py:374
  96.4 0.6 slice.3
  97.6 1.3 %select_add_fusion = f32[2048,128]{1,0:T(8,128)} fusion(f32[2048,128]{1,0:T(8,128)S(1)} %get-tuple-element.7, f32[]{:T(128)S(6)} %mul.25, s32[128]{0:T(128)S(1)} %iota_add_fusion.1, s32[2048]{0:T(1024)S(1)} %iota_add_fusion), kind=kLoop, calls=%fused_computation.1 | loop fusion | flops 1048576 | bytes 2105860 | tf_op jit(solution)/shard_map/add | solution.py:402
  (2 shorter events, 0.0 us)
Async XLA Ops:
  6.7 0.8 copy-start
  7.6 0.7 copy-start.1

commit v3 on v2

v3 whole, which is shorter than its diff:
```python
import math

import jax
import jax.numpy as jnp
from jax import lax
from jax.experimental import pallas as pl
from jax.experimental.pallas import tpu as pltpu
from jax.sharding import Mesh
from jax.sharding import PartitionSpec as P

D = 8192
BLOCK = 32
TOKENS = 6144
COL = ("z", "x", "c")
NY, NZ, NX, NC = 4, 8, 4, 2
TG = TOKENS // (NY * NX)
TT = 128
NT3 = TG // TT
HOPS = (4, 1, 7, 2, 6, 3, 5)
MESH = pl.DeviceIdType.MESH
NT = (((1,), (1,)), ((), ()))
NN = (((1,), (0,)), ((), ()))


def parity_sign(v):
    v = v ^ (v >> 4)
    v = v ^ (v >> 2)
    v = v ^ (v >> 1)
    return 1 - 2 * (v & 1)


def inner_table():
    r = lax.broadcasted_iota(jnp.int32, (128, 128), 0)
    k = lax.broadcasted_iota(jnp.int32, (128, 128), 1)
    b_r = ((r >> 4) << 2) | (r & 3)
    sign = parity_sign(b_r & (k & 31))
    return jnp.where(((r >> 2) & 3) == (k >> 5), sign, 0)


def outer_table(core, for_rows):
    r = lax.broadcasted_iota(jnp.int32, (512, 1), 0)
    k = lax.broadcasted_iota(jnp.int32, (1, 1024), 1)
    if for_rows:
        c = ((r >> 7) << 6) | ((r & 7) << 3) | ((r >> 5) & 3)
        b_r = (r >> 3) & 3
    else:
        c = ((r >> 6) << 5) | (((r >> 4) & 3) << 3) | ((r >> 2) & 3)
        b_r = r & 3
    c = c | (core << 2)
    a = (((k >> 4) & 7) << 5) | (((k >> 7) & 3) << 3) | ((k >> 9) << 2) | ((k >> 2) & 3)
    sign = parity_sign(c & a)
    return jnp.where(b_r == (k & 3), sign, 0).astype(jnp.float32).astype(jnp.bfloat16)


def column_order():
    o = lax.broadcasted_iota(jnp.int32, (128, 128), 0)
    i = lax.broadcasted_iota(jnp.int32, (128, 128), 1)
    src = (((o >> 2) & 7) << 4) | ((o >> 5) << 2) | (o & 3)
    return (i == src).astype(jnp.float32).astype(jnp.bfloat16)


def kernel(
    picked, signs_any, out, tr,
    signs, signs_sem, hb, x1, x2, hm, hn, rm, rn, mb, nz, np_, g, ra, rb, ts, trx,
    s1, r1, s2, r2, s3, r3, sn, rn_sem, sm, rm_sem, sy, ry, sr, rr, sl, rl, sd, rd,
    sa, ra_sem, sb, rb_sem, st, rt,
):
    y, z, x, c = (lax.axis_index(n) for n in ("tok", "z", "x", "c"))
    scale = 1.0 / math.sqrt(D)

    def at_x(d):
        return lax.rem(x + d + NX, NX)

    def at_y(d):
        return lax.rem(y + d + NY, NY)

    def at_z(d):
        return lax.rem(z + d + NZ, NZ)

    def copy(src, dst, send, recv, **where):
        return pltpu.make_async_remote_copy(
            src_ref=src, dst_ref=dst, send_sem=send, recv_sem=recv,
            device_id=where, device_id_type=MESH,
        )

    started = []

    def send(*args, **where):
        cp = copy(*args, **where)
        cp.start()
        started.append(cp)

    def arrived(ref, sem):
        copy(ref, ref, sem, sem, c=1 - c).wait_recv()

    barrier = pltpu.get_barrier_semaphore()
    peers = (
        [dict(x=at_x(d)) for d in range(1, NX)]
        + [dict(tok=at_y(d)) for d in range(1, NY)]
        + [dict(z=at_z(d)) for d in range(1, NZ)]
        + [dict(c=1 - c)]
    )
    for where in peers:
        pl.semaphore_signal(barrier, inc=1, device_id=where, device_id_type=MESH)

    fetch = pltpu.make_async_copy(signs_any, signs, signs_sem)
    fetch.start()
    table = inner_table()
    fetch.wait()
    signed = (table * signs[...]).astype(jnp.float32).astype(jnp.bfloat16)

    def piece(t, zz):
        return hb.at[t, :, pl.ds(pl.multiple_of(zz * 16, 16), 16), :]

    for t in range(NT3):
        for j in range(NX):
            first = j * TG + t * TT
            h = lax.dot_general(
                signed, picked[first : first + TT, :], NT, preferred_element_type=jnp.float32
            )
            hb[t, j] = h.astype(jnp.bfloat16)
        if t == 0:
            pl.semaphore_wait(barrier, len(peers))
        for d in HOPS:
            send(piece(t, at_z(d)), x1.at[t, z], s2.at[t, d - 1], r2.at[t, d - 1], z=at_z(d))
        x1[t, z] = hb[t, :, pl.ds(pl.multiple_of(z * 16, 16), 16), :]
    hn[...] = outer_table(c, False)
    hm[...] = outer_table(c, True)

    def exchange(t):
        for d in HOPS:
            arrived(x1.at[t, at_z(-d)], r2.at[t, d - 1])
        for d in (2, 1, 3):
            send(
                x1.at[t, :, at_x(d)], x2.at[t, c, x], s1.at[t, d - 1], r1.at[t, d - 1], x=at_x(d)
            )
        send(x1.at[t, :, x], x2.at[t, c, x], s3.at[t, 0], r3.at[t, 0], c=1 - c)
        x2[t, c, x] = x1[t, :, x]

    def share_turned(t):
        for d in (1, 3, 2):
            got = x2.at[t, c, at_x(-d)]
            arrived(got, r1.at[t, d - 1])
            send(got, got, s3.at[t, d], r3.at[t, d], c=1 - c)

    def turn(t):
        for d in range(NX):
            arrived(x2.at[t, 1 - c, at_x(-d)], r3.at[t, d])
        spread = x2[t].reshape(1024, TT)

        def times(table):
            return (
                lax.dot_general(table[...], spread, NN, preferred_element_type=jnp.float32) * scale
            ).astype(jnp.bfloat16)

        rn[t] = times(hn).reshape(NZ, 64, TT)
        for d in HOPS:
            send(
                rn.at[t, at_z(d)], nz.at[z, y, t], sn.at[t, d - 1], rn_sem.at[t, d - 1], z=at_z(d)
            )
        nz[z, y, t] = rn[t, z]
        rows = times(hm)
        rm[t] = rows.reshape(NY, 128, TT)
        for d in range(1, NY):
            send(
                rm.at[t, at_y(d)], mb.at[z, c, y, t], sm.at[t, d - 1], rm_sem.at[t, d - 1],
                tok=at_y(d),
            )
        mb[z, c, y, t] = rm[t, y]
        sq = rows.astype(jnp.float32)
        return jnp.sum((sq * sq).reshape(64, 8, TT), axis=0)

    def near(t, d):
        got = nz.at[at_z(-d), y, t]
        send(got, got, sy.at[t, d, 0], ry.at[t, d, 0], tok=at_y(1))
        send(got, got, sy.at[t, d, 1], ry.at[t, d, 1], tok=at_y(-1))

    def far(t, d):
        left, right = nz.at[at_z(-d), at_y(-1), t], nz.at[at_z(-d), at_y(1), t]
        arrived(left, ry.at[t, d, 0])
        arrived(right, ry.at[t, d, 1])
        if (t + d) % 2 == 0:
            send(left, left, sy.at[t, d, 2], ry.at[t, d, 2], tok=at_y(1))
        else:
            send(right, right, sy.at[t, d, 2], ry.at[t, d, 2], tok=at_y(-1))

    stages = [
        [dict(c=1 - c)],
        [dict(x=at_x(d)) for d in range(1, NX)],
        [dict(tok=at_y(d)) for d in range(1, NY)],
        [dict(z=at_z(d)) for d in range(1, NZ)],
    ]
    base = [0, 1, 4, 7]

    def trace_send(k):
        for i, where in enumerate(stages[k]):
            j = base[k] + i
            send(ts.at[k], trx.at[j], st.at[j], rt.at[j], **where)

    def trace_take(k):
        total = ts[k]
        for i in range(len(stages[k])):
            j = base[k] + i
            arrived(trx.at[j], rt.at[j])
            total = total + trx[j]
        return total

    def ring(back, ahead, s, e):
        f = at_y(-e)
        if s < 4 or e < 2:
            got = mb.at[back, c, f]
            send(got, got, sr.at[s - 1, e], rr.at[s - 1, e], z=at_z(1))
        if s < 4 or e >= 2:
            got = mb.at[ahead, c, f]
            send(got, got, sl.at[s - 1, e], rl.at[s - 1, e], z=at_z(-1))

    def share(slot, k, e):
        got = mb.at[slot, c, at_y(-e)]
        send(got, got, sd.at[k, e], rd.at[k, e], c=1 - c)

    def ring_take(s, e):
        back, ahead, f = at_z(-s), at_z(s), at_y(-e)
        if s < 4 or e < 2:
            arrived(mb.at[back, c, f], rr.at[s - 1, e])
        if s < 4 or e >= 2:
            arrived(mb.at[ahead, c, f], rl.at[s - 1, e])
        if s < 4:
            ring(back, ahead, s + 1, e)
            share(back, 2 * s - 1, e)
            share(ahead, 2 * s, e)
        else:
            share(back, 7, e)

    exchange(0)
    exchange(1)
    share_turned(0)
    exchange(2)
    sq = turn(0)
    share_turned(1)
    sq = sq + turn(1)
    near(0, 0)
    share_turned(2)
    sq = sq + turn(2)
    near(1, 0)
    near(2, 0)
    ts[0] = sq
    trace_send(0)
    for e in range(NY):
        if e:
            for t in range(NT3):
                arrived(mb.at[z, c, at_y(-e), t], rm_sem.at[t, e - 1])
        ring(z, z, 1, e)
        share(z, 0, e)
    for t in range(NT3):
        for d in HOPS:
            arrived(nz.at[at_z(-d), y, t], rn_sem.at[t, d - 1])
            near(t, d)
        if t == 0:
            for e in range(NT3):
                far(e, 0)
        else:
            for d in HOPS:
                far(t - 1, d)
    ring_take(1, 0)
    for d in HOPS:
        far(NT3 - 1, d)
    ts[1] = trace_take(0)
    trace_send(1)
    ring_take(1, 1)

    order = column_order()
    for t in range(NT3):
        for d in range(NZ):
            arrived(nz.at[at_z(-d), at_y(2), t], ry.at[t, d, 2])
        for e in range(NY):
            lane = e * TG + t * TT
            for j in range(NX):
                part = nz[:, e, t, j * 16 : (j + 1) * 16, :].reshape(128, TT)
                np_[j * 128 : (j + 1) * 128, lane : lane + TT] = lax.dot_general(
                    order, part, NN, preferred_element_type=jnp.float32
                ).astype(jnp.bfloat16)

    slots = [z, at_z(-1), at_z(1), at_z(-2), at_z(2), at_z(-3), at_z(3), at_z(4)]
    right, left = at_x(1), at_x(-1)

    def multiply(k):
        slot = slots[k]
        for e in range(NY):
            arrived(mb.at[slot, 1 - c, at_y(-e)], rd.at[k, e])
        lhs = jnp.concatenate(
            [
                jnp.concatenate(
                    [mb[slot, e, f, t] for f in range(NY) for t in range(NT3)], axis=1
                )
                for e in range(NC)
            ],
            axis=0,
        )
        prod = lax.dot_general(lhs, np_[...], NT, preferred_element_type=jnp.float32)
        for j in range(NX):
            g[k, j] = prod[:, j * 128 : (j + 1) * 128]
        apart = g.at[k, at_x(2)]
        send(apart.at[0:128], ra.at[k, 0], sa.at[k, 0], ra_sem.at[k, 0], x=right)
        send(apart.at[128:256], ra.at[k, 1], sa.at[k, 1], ra_sem.at[k, 1], x=left)
        hand(k, 0, 1)
        hand(k, 1, 0)

    def hand(k, side, half):
        to = (right, left)[side]
        src = g.at[k, to, half * 128 : half * 128 + 128]
        send(
            src, rb.at[k, side, half], sb.at[k, side, half], rb_sem.at[k, side, half], x=to
        )

    def pass_on(k):
        for side, to in ((0, right), (1, left)):
            arrived(ra.at[k, side], ra_sem.at[k, side])
            rows = slice(side * 128, side * 128 + 128)
            g[k, to, rows, :] = g[k, to, rows, :] + ra[k, side]
            hand(k, side, side)

    def finish(k):
        for half in (1, 0):
            arrived(rb.at[k, half, 1 - half], rb_sem.at[k, half, 1 - half])
        for half in range(2):
            arrived(rb.at[k, half, half], rb_sem.at[k, half, half])
        for half in range(2):
            rows = slice(half * 128, half * 128 + 128)
            total = g[k, x, rows, :] + rb[k, 0, half] + rb[k, 1, half]
            for i in range(16):
                start = half * 128 + (i >> 2) * 32 + (i & 3) + slots[k] * 4
                out[pl.ds(start, 8, stride=256), :] = total[i * 8 : (i + 1) * 8, :]

    multiply(0)
    ring_take(1, 2)
    ring_take(1, 3)
    multiply(1)
    pass_on(0)
    multiply(2)
    for s in range(1, 4):
        ring_take(s + 1, 0)
        pass_on(2 * s - 1)
        ring_take(s + 1, 1)
        if s == 1:
            finish(0)
        pass_on(2 * s)
        ring_take(s + 1, 2)
        finish(2 * s - 1)
        ring_take(s + 1, 3)
        multiply(2 * s + 1)
        if s < 3:
            multiply(2 * s + 2)
            ts[s + 1] = trace_take(s)
            trace_send(s + 1)
        finish(2 * s)
    pass_on(7)
    tr[...] = jnp.full((8, 128), jnp.sum(trace_take(3)), jnp.float32)
    finish(7)
    for cp in started:
        cp.wait_send()


def rotate_and_multiply(picked, signs):
    bf, f32 = jnp.bfloat16, jnp.float32
    V = pltpu.VMEM
    dma = pltpu.SemaphoreType.DMA
    scratch = [
        V((1, 128), jnp.int32),
        dma(()),
        V((NT3, NX, 128, TT), bf),
        V((NT3, NZ, NX, 16, TT), bf),
        V((NT3, NC, NX, NZ, 16, TT), bf),
        V((512, 1024), bf),
        V((512, 1024), bf),
        V((NT3, NY, 128, TT), bf),
        V((NT3, NZ, 64, TT), bf),
        V((NZ, NC, NY, NT3, 128, TT), bf),
        V((NZ, NY, NT3, 64, TT), bf),
        V((512, NY * TG), bf),
        V((NZ, NX, 256, 128), f32),
        V((NZ, 2, 128, 128), f32),
        V((NZ, 2, 2, 128, 128), f32),
        V((4, 8, 128), f32),
        V((14, 8, 128), f32),
    ] + [
        dma(shape)
        for shape in (
            (NT3, 3), (NT3, 7), (NT3, 4), (NT3, 7), (NT3, 3), (NT3, 8, 3),
            (4, 4), (4, 4), (8, 4), (8, 2), (8, 2, 2), (14,),
        )
        for _ in range(2)
    ]
    vmem = pl.BlockSpec(memory_space=pltpu.VMEM)
    return pl.pallas_call(
        kernel,
        out_shape=(
            jax.ShapeDtypeStruct((2048, 128), f32),
            jax.ShapeDtypeStruct((8, 128), f32),
        ),
        in_specs=[vmem, pl.BlockSpec(memory_space=pltpu.MemorySpace.HBM)],
        out_specs=(vmem, vmem),
        scratch_shapes=scratch,
        compiler_params=pltpu.CompilerParams(
            collective_id=0, has_side_effects=True, vmem_limit_bytes=48 * 1024 * 1024
        ),
    )(picked, signs)


def shards(row_bank, token_ids, sign_flips, damping):
    picked = lax.gather(
        row_bank,
        token_ids[:, None],
        lax.GatherDimensionNumbers((1,), (0,), (0,)),
        (1, row_bank.shape[1]),
        mode=lax.GatherScatterMode.PROMISE_IN_BOUNDS,
    )
    gram, squares = rotate_and_multiply(picked, sign_flips[None, :])
    mean_diag = squares[:1, :] / TOKENS / D
    row_index = lax.axis_index("tok") * 2048 + lax.broadcasted_iota(jnp.int32, gram.shape, 0)
    col_index = lax.axis_index(COL) * 128 + lax.broadcasted_iota(jnp.int32, gram.shape, 1)
    on_diag = (row_index == col_index).astype(jnp.float32)
    return gram / TOKENS + damping[0] * mean_diag * on_diag


def solution(mesh):
    split = Mesh(mesh.devices.reshape(NY, NZ, NX, NC), ("tok",) + COL)
    return jax.shard_map(
        shards,
        mesh=split,
        in_specs=(P(None, COL), P("tok"), P(COL), P()),
        out_specs=P("tok", COL),
        check_vma=False,
    )
```

time: 99.1 us -> 105 us (1.060)
  Pallas kernels: 88.1 us -> 95.7 us
  local copies, waits for them, and re-layouts: 7.43 us -> 6.01 us
    pallas_call x1, Pallas kernels: 88.1 us -> 95.7 us  [rotate_and_multiply(): pl.pallas_call(kernel, out_shape=(jax.ShapeDtypeStruct((2048, 128), f32),...]
where the time goes in v3:
time: 105 us; the launch traced here: 104 us
  Pallas kernels  95.7 us (91%)
  local copies, waits for them, and re-layouts  6.01 us (6%)
  other arithmetic  2.03 us (2%)
    pallas_call x1, Pallas kernels, rotate_and_multiply(): pl.pallas_call(kernel, out_shape=(jax.ShapeDtypeStruct((2048, 128), f32),...  95.7 us
    gather x1, local copies, waits for them, and re-layouts, shards(): lax.gather(row_bank, token_ids[:, None], lax.GatherDimensionNumbers((1,),...  5.36 us

profile of v3, /device:TPU:1, one launch (start us, length us, event | category | flops | bytes accessed | tf_op | source)
XLA Modules:
  0.0 104.5 jit_solution(3995701153658840218)
XLA Ops:
  0.7 0.7 pad_clamp_fusion
  1.4 5.4 %gather_fusion = bf16[1536,128]{1,0:T(8,128)(2,1)S(1)} fusion(bf16[16384,128]{1,0:T(8,128)(2,1)} %param.4, s32[2048]{0:T(1024)S(1)} %pad_clamp_fusion), kind=kCustom, calls=%fused_computation | custom fusion | bytes 792576 | tf_op jit(solution)/shard_map/gather | solution.py:410
  6.7 0.0 copy-start
  6.8 0.6 copy-done
  7.4 95.7 %shard_map.46 = (f32[2048,128]{1,0:T(8,128)S(1)}, f32[8,128]{1,0:T(8,128)S(1)}) custom-call(bf16[1536,128]{1,0:T(8,128)(2,1)S(1)} %gather_fusion, s32[1,128]{1,0:T(1,128)S(1)} %bitcast.4), custom_call_target="tpu_custom_call" | custom-call | tf_op jit(solution)/shard_map/pallas_call | solution.py:394
  103.2 1.3 %select_add_fusion = f32[2048,128]{1,0:T(8,128)} fusion(f32[2048,128]{1,0:T(8,128)S(1)} %get-tuple-element.7, f32[128]{0:T(128)S(1)} %multiply_bitcast_fusion, s32[128]{0:T(128)S(1)} %iota_add_fusion.1, s32[2048]{0:T(1024)S(1)} %iota_add_fusion), kind=kLoop, calls=%fused_computation.1 | loop fusion | flops 1048576 | bytes 2106368 | tf_op jit(solution)/shard_map/add | solution.py:422
  (3 shorter events, 0.0 us)
Async XLA Ops:
  6.7 0.7 copy-start

commit v4 on v3

--- a/solution.py
+++ b/solution.py
@@ -16,7 +16,8 @@
 TG = TOKENS // (NY * NX)
 TT = 128
 NT3 = TG // TT
-HOPS = (4, 1, 7, 2, 6, 3, 5)
+HOPS = (4, 3, 5, 2, 6, 1, 7)
+TILES = (1, 2, 0)
 MESH = pl.DeviceIdType.MESH
 NT = (((1,), (1,)), ((), ()))
 NN = (((1,), (0,)), ((), ()))
@@ -38,18 +39,25 @@
 
 
 def outer_table(core, for_rows):
-    r = lax.broadcasted_iota(jnp.int32, (512, 1), 0)
     k = lax.broadcasted_iota(jnp.int32, (1, 1024), 1)
+    a = (((k >> 4) & 7) << 5) | (((k >> 7) & 3) << 3) | ((k >> 9) << 2) | ((k >> 2) & 3)
+
+    def bits(r):
+        if for_rows:
+            return ((r >> 7) << 6) | ((r & 7) << 3) | ((r >> 5) & 3), (r >> 3) & 3
+        return ((r >> 6) << 5) | (((r >> 4) & 3) << 3) | ((r >> 2) & 3), r & 3
+
+    c_group, b_group = bits(lax.broadcasted_iota(jnp.int32, (64, 1), 0) * 8)
+    c_place, b_place = bits(lax.broadcasted_iota(jnp.int32, (8, 1), 0))
+    group = parity_sign((c_group | (core << 2)) & a)
+    place = parity_sign(c_place & a)
     if for_rows:
-        c = ((r >> 7) << 6) | ((r & 7) << 3) | ((r >> 5) & 3)
-        b_r = (r >> 3) & 3
+        group = jnp.where(b_group == (k & 3), group, 0)
     else:
-        c = ((r >> 6) << 5) | (((r >> 4) & 3) << 3) | ((r >> 2) & 3)
-        b_r = r & 3
-    c = c | (core << 2)
-    a = (((k >> 4) & 7) << 5) | (((k >> 7) & 3) << 3) | ((k >> 9) << 2) | ((k >> 2) & 3)
-    sign = parity_sign(c & a)
-    return jnp.where(b_r == (k & 3), sign, 0).astype(jnp.float32).astype(jnp.bfloat16)
+        place = jnp.where(b_place == (k & 3), place, 0)
+    group, place = group.astype(jnp.float32), place.astype(jnp.float32)
+    table = group[:, None, :] * place[None, :, :]
+    return table.reshape(512, 1024).astype(jnp.bfloat16)
 
 
 def column_order():
@@ -60,8 +68,8 @@
 
 
 def kernel(
-    picked, signs_any, out, tr,
-    signs, signs_sem, hb, x1, x2, hm, hn, rm, rn, mb, nz, np_, g, ra, rb, ts, trx,
+    damping, picked, signs_any, out,
+    signs, signs_sem, xf, hb, x1, x2, hm, hn, rm, rn, mb, nz, np_, g, ra, rb, ts, trx,
     s1, r1, s2, r2, s3, r3, sn, rn_sem, sm, rm_sem, sy, ry, sr, rr, sl, rl, sd, rd,
     sa, ra_sem, sb, rb_sem, st, rt,
 ):
@@ -119,17 +127,42 @@
                 signed, picked[first : first + TT, :], NT, preferred_element_type=jnp.float32
             )
             hb[t, j] = h.astype(jnp.bfloat16)
-        if t == 0:
-            pl.semaphore_wait(barrier, len(peers))
+
+    def scatter(t):
         for d in HOPS:
             send(piece(t, at_z(d)), x1.at[t, z], s2.at[t, d - 1], r2.at[t, d - 1], z=at_z(d))
         x1[t, z] = hb[t, :, pl.ds(pl.multiple_of(z * 16, 16), 16), :]
-    hn[...] = outer_table(c, False)
-    hm[...] = outer_table(c, True)
+
+    def take(t, hops):
+        for d in hops:
+            arrived(x1.at[t, at_z(-d)], r2.at[t, d - 1])
+
+    pl.semaphore_wait(barrier, len(peers))
+
+    def scatter_x():
+        for d in (2, 1, 3):
+            send(hb.at[0, at_x(d)], xf.at[x], s1.at[0, d - 1], r1.at[0, d - 1], x=at_x(d))
+        xf[x] = hb[0, x]
+
+    def part_z(zz):
+        return xf.at[:, pl.ds(pl.multiple_of(zz * 16, 16), 16), :]
+
+    def scatter_z():
+        for d in range(1, NX):
+            arrived(xf.at[at_x(-d)], r1.at[0, d - 1])
+        mine = x2.at[0, c, :, z]
+        for d in HOPS:
+            send(part_z(at_z(d)), mine, s2.at[0, d - 1], r2.at[0, d - 1], z=at_z(d))
+        send(part_z(z), mine, s3.at[0, 0], r3.at[0, 0], c=1 - c)
+        x2[0, c, :, z] = xf[:, pl.ds(pl.multiple_of(z * 16, 16), 16), :]
+
+    def share_z():
+        for d in HOPS:
+            got = x2.at[0, c, :, at_z(-d)]
+            arrived(got, r2.at[0, d - 1])
+            send(got, got, s3.at[0, d], r3.at[0, d], c=1 - c)
 
     def exchange(t):
-        for d in HOPS:
-            arrived(x1.at[t, at_z(-d)], r2.at[t, d - 1])
         for d in (2, 1, 3):
             send(
                 x1.at[t, :, at_x(d)], x2.at[t, c, x], s1.at[t, d - 1], r1.at[t, d - 1], x=at_x(d)
@@ -144,8 +177,9 @@
             send(got, got, s3.at[t, d], r3.at[t, d], c=1 - c)
 
     def turn(t):
-        for d in range(NX):
-            arrived(x2.at[t, 1 - c, at_x(-d)], r3.at[t, d])
+        for d in range(NX if t else NZ):
+            theirs = x2.at[t, 1 - c, at_x(-d)] if t else x2.at[t, 1 - c, :, at_z(-d)]
+            arrived(theirs, r3.at[t, d])
         spread = x2[t].reshape(1024, TT)
 
         def times(table):
@@ -231,18 +265,25 @@
         else:
             share(back, 7, e)
 
-    exchange(0)
+    scatter_x()
+    scatter(1)
+    scatter(2)
+    hn[...] = outer_table(c, False)
+    hm[...] = outer_table(c, True)
+    scatter_z()
+    take(1, HOPS)
     exchange(1)
-    share_turned(0)
+    take(2, HOPS)
     exchange(2)
-    sq = turn(0)
     share_turned(1)
-    sq = sq + turn(1)
-    near(0, 0)
+    sq = turn(1)
+    near(1, 0)
+    share_z()
     share_turned(2)
     sq = sq + turn(2)
-    near(1, 0)
     near(2, 0)
+    sq = sq + turn(0)
+    near(0, 0)
     ts[0] = sq
     trace_send(0)
     for e in range(NY):
@@ -251,25 +292,35 @@
                 arrived(mb.at[z, c, at_y(-e), t], rm_sem.at[t, e - 1])
         ring(z, z, 1, e)
         share(z, 0, e)
-    for t in range(NT3):
+    def land(t):
         for d in HOPS:
             arrived(nz.at[at_z(-d), y, t], rn_sem.at[t, d - 1])
             near(t, d)
-        if t == 0:
-            for e in range(NT3):
-                far(e, 0)
-        else:
-            for d in HOPS:
-                far(t - 1, d)
+
+    def relay_own():
+        for t in TILES:
+            far(t, 0)
+
+    def relay(t):
+        for d in HOPS:
+            far(t, d)
+
+    land(1)
+    relay_own()
+    land(2)
+    relay(1)
+    land(0)
     ring_take(1, 0)
-    for d in HOPS:
-        far(NT3 - 1, d)
+    relay(2)
+    ring_take(1, 1)
+    relay(0)
+    ring_take(1, 2)
+    ring_take(1, 3)
     ts[1] = trace_take(0)
     trace_send(1)
-    ring_take(1, 1)
 
     order = column_order()
-    for t in range(NT3):
+    for t in TILES:
         for d in range(NZ):
             arrived(nz.at[at_z(-d), at_y(2), t], ry.at[t, d, 2])
         for e in range(NY):
@@ -332,41 +383,64 @@
                 out[pl.ds(start, 8, stride=256), :] = total[i * 8 : (i + 1) * 8, :]
 
     multiply(0)
-    ring_take(1, 2)
-    ring_take(1, 3)
     multiply(1)
+    multiply(2)
+    ring_take(2, 0)
     pass_on(0)
-    multiply(2)
-    for s in range(1, 4):
-        ring_take(s + 1, 0)
-        pass_on(2 * s - 1)
-        ring_take(s + 1, 1)
-        if s == 1:
-            finish(0)
-        pass_on(2 * s)
-        ring_take(s + 1, 2)
-        finish(2 * s - 1)
-        ring_take(s + 1, 3)
-        multiply(2 * s + 1)
-        if s < 3:
-            multiply(2 * s + 2)
-            ts[s + 1] = trace_take(s)
-            trace_send(s + 1)
-        finish(2 * s)
+    ring_take(2, 1)
+    pass_on(1)
+    ring_take(2, 2)
+    ring_take(2, 3)
+    multiply(3)
+    multiply(4)
+    ring_take(3, 0)
+    finish(0)
+    pass_on(2)
+    ring_take(3, 1)
+    finish(1)
+    ring_take(3, 2)
+    pass_on(3)
+    ring_take(3, 3)
+    multiply(5)
+    finish(2)
+    multiply(6)
+    ring_take(4, 0)
+    pass_on(4)
+    ring_take(4, 1)
+    finish(3)
+    ring_take(4, 2)
+    pass_on(5)
+    ring_take(4, 3)
+    multiply(7)
+    ts[2] = trace_take(1)
+    trace_send(2)
+    finish(4)
+    pass_on(6)
+    ts[3] = trace_take(2)
+    trace_send(3)
+    finish(5)
     pass_on(7)
-    tr[...] = jnp.full((8, 128), jnp.sum(trace_take(3)), jnp.float32)
+    trace = jnp.sum(trace_take(3))
+    finish(6)
     finish(7)
+
+    i = lax.broadcasted_iota(jnp.int32, (128, 128), 0)
+    j = lax.broadcasted_iota(jnp.int32, (128, 128), 1)
+    block = pl.ds(pl.multiple_of(((z & 1) * 8 + x * 2 + c) * 128, 128), 128)
+    on_diag = jnp.where((i == j) & (y == (z >> 1)), damping[0] * (trace / D), 0.0)
+    out[block, :] = out[block, :] + on_diag
     for cp in started:
         cp.wait_send()
 
 
-def rotate_and_multiply(picked, signs):
+def rotate_and_multiply(damping, picked, signs):
     bf, f32 = jnp.bfloat16, jnp.float32
     V = pltpu.VMEM
     dma = pltpu.SemaphoreType.DMA
     scratch = [
         V((1, 128), jnp.int32),
         dma(()),
+        V((NX, 128, TT), bf),
         V((NT3, NX, 128, TT), bf),
         V((NT3, NZ, NX, 16, TT), bf),
         V((NT3, NC, NX, NZ, 16, TT), bf),
@@ -385,25 +459,24 @@
     ] + [
         dma(shape)
         for shape in (
-            (NT3, 3), (NT3, 7), (NT3, 4), (NT3, 7), (NT3, 3), (NT3, 8, 3),
+            (NT3, 3), (NT3, 7), (NT3, 8), (NT3, 7), (NT3, 3), (NT3, 8, 3),
             (4, 4), (4, 4), (8, 4), (8, 2), (8, 2, 2), (14,),
         )
         for _ in range(2)
     ]
     vmem = pl.BlockSpec(memory_space=pltpu.VMEM)
+    smem = pl.BlockSpec(memory_space=pltpu.SMEM)
+    hbm = pl.BlockSpec(memory_space=pltpu.MemorySpace.HBM)
     return pl.pallas_call(
         kernel,
-        out_shape=(
-            jax.ShapeDtypeStruct((2048, 128), f32),
-            jax.ShapeDtypeStruct((8, 128), f32),
-        ),
-        in_specs=[vmem, pl.BlockSpec(memory_space=pltpu.MemorySpace.HBM)],
-        out_specs=(vmem, vmem),
+        out_shape=jax.ShapeDtypeStruct((2048, 128), f32),
+        in_specs=[smem, vmem, hbm],
+        out_specs=vmem,
         scratch_shapes=scratch,
         compiler_params=pltpu.CompilerParams(
             collective_id=0, has_side_effects=True, vmem_limit_bytes=48 * 1024 * 1024
         ),
-    )(picked, signs)
+    )(damping, picked, signs)
 
 
 def shards(row_bank, token_ids, sign_flips, damping):
@@ -414,12 +487,7 @@
         (1, row_bank.shape[1]),
         mode=lax.GatherScatterMode.PROMISE_IN_BOUNDS,
     )
-    gram, squares = rotate_and_multiply(picked, sign_flips[None, :])
-    mean_diag = squares[:1, :] / TOKENS / D
-    row_index = lax.axis_index("tok") * 2048 + lax.broadcasted_iota(jnp.int32, gram.shape, 0)
-    col_index = lax.axis_index(COL) * 128 + lax.broadcasted_iota(jnp.int32, gram.shape, 1)
-    on_diag = (row_index == col_index).astype(jnp.float32)
-    return gram / TOKENS + damping[0] * mean_diag * on_diag
+    return rotate_and_multiply(damping, picked, sign_flips[None, :]) / TOKENS
 
 
 def solution(mesh):

time: 105 us -> 94.9 us (0.904)
  Pallas kernels: 95.7 us -> 86.3 us
    pallas_call x1, Pallas kernels: 95.7 us -> 86.3 us  [rotate_and_multiply(): pl.pallas_call(kernel, out_shape=jax.ShapeDtypeStruct((2048, 128), f32),...]
    add x3 -> x0, other arithmetic: 1.32 us -> none  [the longest x1 1.31 us: shards(): return gram / TOKENS + damping[0] * mean_diag * on_diag]
    div x0 -> x1, other arithmetic: none -> 1.06 us  [shards(): return rotate_and_multiply(damping, picked, sign_flips[None, :]) / TOKENS]
where the time goes in v4:
time: 94.9 us; the launch traced here: 94.8 us
  Pallas kernels  86.3 us (91%)
  local copies, waits for them, and re-layouts  6.01 us (6%)
  other arithmetic  1.77 us (2%)
    pallas_call x1, Pallas kernels, rotate_and_multiply(): pl.pallas_call(kernel, out_shape=jax.ShapeDtypeStruct((2048, 128), f32),...  86.3 us
    gather x1, local copies, waits for them, and re-layouts, shards(): lax.gather(row_bank, token_ids[:, None], lax.GatherDimensionNumbers((1,),...  5.36 us

profile of v4, /device:TPU:1, one launch (start us, length us, event | category | flops | bytes accessed | tf_op | source)
XLA Modules:
  0.0 94.8 jit_solution(15919215833489908902)
XLA Ops:
  0.7 0.7 pad_clamp_fusion
  1.4 5.4 %gather_fusion = bf16[1536,128]{1,0:T(8,128)(2,1)S(1)} fusion(bf16[16384,128]{1,0:T(8,128)(2,1)} %param.4, s32[2048]{0:T(1024)S(1)} %pad_clamp_fusion), kind=kCustom, calls=%fused_computation | custom fusion | bytes 792576 | tf_op jit(solution)/shard_map/gather | solution.py:483
  6.7 0.0 copy-start
  6.7 0.6 copy-done
  7.4 86.3 %shard_map.46 = f32[2048,128]{1,0:T(8,128)S(1)} custom-call(f32[1]{0:T(128)S(6)} %copy.5.damping, bf16[1536,128]{1,0:T(8,128)(2,1)S(1)} %gather_fusion, s32[1,128]{1,0:T(1,128)S(1)} %bitcast.1), custom_call_target="tpu_custom_call" | custom-call | tf_op jit(solution)/shard_map/pallas_call | solution.py:470
  93.7 1.1 %broadcast_multiply_fusion = f32[2048,128]{1,0:T(8,128)} fusion(f32[2048,128]{1,0:T(8,128)S(1)} %shard_map.46), kind=kLoop, calls=%fused_computation.1 | loop fusion | flops 262144 | bytes 2097152 | tf_op jit(solution)/shard_map/div | solution.py:490
Async XLA Ops:
  6.7 0.7 copy-start

commit v5 on v4

--- a/solution.py
+++ b/solution.py
@@ -268,9 +268,9 @@
     scatter_x()
     scatter(1)
     scatter(2)
+    scatter_z()
     hn[...] = outer_table(c, False)
     hm[...] = outer_table(c, True)
-    scatter_z()
     take(1, HOPS)
     exchange(1)
     take(2, HOPS)
@@ -386,40 +386,40 @@
     multiply(1)
     multiply(2)
     ring_take(2, 0)
+    ring_take(2, 1)
+    ring_take(2, 2)
     pass_on(0)
-    ring_take(2, 1)
-    pass_on(1)
-    ring_take(2, 2)
     ring_take(2, 3)
     multiply(3)
     multiply(4)
+    pass_on(1)
     ring_take(3, 0)
+    ring_take(3, 1)
     finish(0)
     pass_on(2)
-    ring_take(3, 1)
-    finish(1)
     ring_take(3, 2)
-    pass_on(3)
     ring_take(3, 3)
     multiply(5)
+    multiply(6)
+    pass_on(3)
+    finish(1)
+    ring_take(4, 0)
+    ring_take(4, 1)
+    pass_on(4)
     finish(2)
-    multiply(6)
-    ring_take(4, 0)
-    pass_on(4)
-    ring_take(4, 1)
-    finish(3)
     ring_take(4, 2)
-    pass_on(5)
     ring_take(4, 3)
     multiply(7)
     ts[2] = trace_take(1)
     trace_send(2)
+    pass_on(5)
+    finish(3)
+    pass_on(6)
     finish(4)
-    pass_on(6)
     ts[3] = trace_take(2)
     trace_send(3)
+    pass_on(7)
     finish(5)
-    pass_on(7)
     trace = jnp.sum(trace_take(3))
     finish(6)
     finish(7)

time: 94.9 us -> 93.7 us (0.987)
  Pallas kernels: 86.3 us -> 85 us
    pallas_call x1, Pallas kernels: 86.3 us -> 85 us  [rotate_and_multiply(): pl.pallas_call(kernel, out_shape=jax.ShapeDtypeStruct((2048, 128), f32),...]
where the time goes in v5:
time: 93.7 us; the launch traced here: 93.4 us
  Pallas kernels  85 us (91%)
  local copies, waits for them, and re-layouts  6.01 us (6%)
  other arithmetic  1.77 us (2%)
    pallas_call x1, Pallas kernels, rotate_and_multiply(): pl.pallas_call(kernel, out_shape=jax.ShapeDtypeStruct((2048, 128), f32),...  85 us
    gather x1, local copies, waits for them, and re-layouts, shards(): lax.gather(row_bank, token_ids[:, None], lax.GatherDimensionNumbers((1,),...  5.36 us

profile of v5, /device:TPU:1, one launch (start us, length us, event | category | flops | bytes accessed | tf_op | source)
XLA Modules:
  0.0 93.4 jit_solution(7496097923982551308)
XLA Ops:
  0.7 0.7 pad_clamp_fusion
  1.4 5.4 %gather_fusion = bf16[1536,128]{1,0:T(8,128)(2,1)S(1)} fusion(bf16[16384,128]{1,0:T(8,128)(2,1)} %param.4, s32[2048]{0:T(1024)S(1)} %pad_clamp_fusion), kind=kCustom, calls=%fused_computation | custom fusion | bytes 792576 | tf_op jit(solution)/shard_map/gather | solution.py:483
  6.7 0.0 copy-start
  6.7 0.6 copy-done
  7.4 85.0 %shard_map.46 = f32[2048,128]{1,0:T(8,128)S(1)} custom-call(f32[1]{0:T(128)S(6)} %copy.5.damping, bf16[1536,128]{1,0:T(8,128)(2,1)S(1)} %gather_fusion, s32[1,128]{1,0:T(1,128)S(1)} %bitcast.1), custom_call_target="tpu_custom_call" | custom-call | tf_op jit(solution)/shard_map/pallas_call | solution.py:470
  92.4 1.1 %broadcast_multiply_fusion = f32[2048,128]{1,0:T(8,128)} fusion(f32[2048,128]{1,0:T(8,128)S(1)} %shard_map.46), kind=kLoop, calls=%fused_computation.1 | loop fusion | flops 262144 | bytes 2097152 | tf_op jit(solution)/shard_map/div | solution.py:490
Async XLA Ops:
  6.7 0.7 copy-start

commit v6 on v5

--- a/solution.py
+++ b/solution.py
@@ -68,8 +68,8 @@
 
 
 def kernel(
-    damping, picked, signs_any, out,
-    signs, signs_sem, xf, hb, x1, x2, hm, hn, rm, rn, mb, nz, np_, g, ra, rb, ts, trx,
+    damping, picked, signs, out,
+    xf, hb, x1, x2, hm, hn, rm, rn, mb, nz, np_, g, ra, rb, ts, trx,
     s1, r1, s2, r2, s3, r3, sn, rn_sem, sm, rm_sem, sy, ry, sr, rr, sl, rl, sd, rd,
     sa, ra_sem, sb, rb_sem, st, rt,
 ):
@@ -111,11 +111,12 @@
     for where in peers:
         pl.semaphore_signal(barrier, inc=1, device_id=where, device_id_type=MESH)
 
-    fetch = pltpu.make_async_copy(signs_any, signs, signs_sem)
-    fetch.start()
     table = inner_table()
-    fetch.wait()
-    signed = (table * signs[...]).astype(jnp.float32).astype(jnp.bfloat16)
+    lane = lax.broadcasted_iota(jnp.int32, (1, 128), 1)
+    row = jnp.zeros((1, 128), jnp.int32)
+    for i in range(128):
+        row = jnp.where(lane == i, signs[i], row)
+    signed = (table * row).astype(jnp.float32).astype(jnp.bfloat16)
 
     def piece(t, zz):
         return hb.at[t, :, pl.ds(pl.multiple_of(zz * 16, 16), 16), :]
@@ -438,8 +439,6 @@
     V = pltpu.VMEM
     dma = pltpu.SemaphoreType.DMA
     scratch = [
-        V((1, 128), jnp.int32),
-        dma(()),
         V((NX, 128, TT), bf),
         V((NT3, NX, 128, TT), bf),
         V((NT3, NZ, NX, 16, TT), bf),
@@ -466,11 +465,10 @@
     ]
     vmem = pl.BlockSpec(memory_space=pltpu.VMEM)
     smem = pl.BlockSpec(memory_space=pltpu.SMEM)
-    hbm = pl.BlockSpec(memory_space=pltpu.MemorySpace.HBM)
     return pl.pallas_call(
         kernel,
         out_shape=jax.ShapeDtypeStruct((2048, 128), f32),
-        in_specs=[smem, vmem, hbm],
+        in_specs=[smem, vmem, smem],
         out_specs=vmem,
         scratch_shapes=scratch,
         compiler_params=pltpu.CompilerParams(
@@ -487,7 +485,7 @@
         (1, row_bank.shape[1]),
         mode=lax.GatherScatterMode.PROMISE_IN_BOUNDS,
     )
-    return rotate_and_multiply(damping, picked, sign_flips[None, :]) / TOKENS
+    return rotate_and_multiply(damping, picked, sign_flips) / TOKENS
 
 
 def solution(mesh):

time: 93.7 us -> 94.4 us (level)
  no operation moved by 1% of the time
where the time goes in v6:
time: 94.4 us; the launch traced here: 93.9 us
  Pallas kernels  85.5 us (91%)
  local copies, waits for them, and re-layouts  6.01 us (6%)
  other arithmetic  1.77 us (2%)
    pallas_call x1, Pallas kernels, rotate_and_multiply(): pl.pallas_call(kernel, out_shape=jax.ShapeDtypeStruct((2048, 128), f32),...  85.5 us
    gather x1, local copies, waits for them, and re-layouts, shards(): lax.gather(row_bank, token_ids[:, None], lax.GatherDimensionNumbers((1,),...  5.36 us

profile of v6, /device:TPU:1, one launch (start us, length us, event | category | flops | bytes accessed | tf_op | source)
XLA Modules:
  0.0 93.9 jit_solution(13393115165905860971)
XLA Ops:
  0.7 0.7 pad_clamp_fusion
  1.4 5.4 %gather_fusion = bf16[1536,128]{1,0:T(8,128)(2,1)S(1)} fusion(bf16[16384,128]{1,0:T(8,128)(2,1)} %param.4, s32[2048]{0:T(1024)S(1)} %pad_clamp_fusion), kind=kCustom, calls=%fused_computation | custom fusion | bytes 792576 | tf_op jit(solution)/shard_map/gather | solution.py:481
  6.7 0.0 copy-start
  6.7 0.6 copy-done
  7.4 85.5 %shard_map.46 = f32[2048,128]{1,0:T(8,128)S(1)} custom-call(f32[1]{0:T(128)S(6)} %copy.5.damping, bf16[1536,128]{1,0:T(8,128)(2,1)S(1)} %gather_fusion, s32[128]{0:T(128)S(1)} %copy-done), custom_call_target="tpu_custom_call" | custom-call | tf_op jit(solution)/shard_map/pallas_call | solution.py:468
  92.9 1.1 %broadcast_multiply_fusion = f32[2048,128]{1,0:T(8,128)} fusion(f32[2048,128]{1,0:T(8,128)S(1)} %shard_map.46), kind=kLoop, calls=%fused_computation.1 | loop fusion | flops 262144 | bytes 2097152 | tf_op jit(solution)/shard_map/div | solution.py:488
Async XLA Ops:
  6.7 0.7 copy-start
